TPU v7x, 32 devices: a whole 2x2x4 slice. The times are simulated.
32 devices in a mesh: blk: 8 (over z, x), grp: 4 (over y, core).
Axes of the slice: x: 2, y: 2, z: 4, core: 2. Of those that a mesh axis runs over, the one named last changes fastest.
Arguments:
- amplitudes: bfloat16 [8, 512, 1024], P('blk', None, 'grp'), may hold values from -6 to 6
- integrals: bfloat16 [64, 1024, 1024], P('blk', 'grp'), may hold values from -0.1875 to 0.1875
- cd_index: int32 [64], replicated, may hold values from 0 to 7, as said below
- live_blocks: int32 [8], replicated, may hold values from 4 to 8, as said below
- occ_energy: float32 [512], P('grp'), may hold values from -3 to -0.5
- vir_energy: float32 [8, 1024], P('blk'), may hold values from 0.5 to 4
Outputs:
- amplitude_step: float32 [8, 512, 1024], P('blk', 'grp')
Inputs may be any that keep to these rules, and one draw needn't show every extreme that they name: (cd_index[k] - k // 8) mod 8 is at most 2 or at least 6; among the first 4 slots of each pair block every nonzero offset from -2 to 2 occurs once. `live_blocks`: 8 is reached by some pair block in every draw.
All inputs are finite; a program needn't handle non-finite values.
Results may differ from a plain program's by a relative error of at most 0.0003.
Values may be sent and summed in bfloat16 or wider, within the bound.
A program may use at most 64 MiB of HBM per device.

v0:
```python
import jax
import jax.numpy as jnp
from jax import lax
from jax.sharding import PartitionSpec as P

REACH = 2


def shifted(value, axis, steps):
    count = lax.axis_size(axis)
    pairs = [(source, (source + steps) % count) for source in range(count)]
    return lax.ppermute(value, axis, pairs)


def cycle_offsets(cd_values, center, cycle_reach, cycle_size):
    return jnp.mod(cd_values - center + cycle_reach, cycle_size)


def contract_tasks(nearby, pieces, offsets, begin_slot, end_slot):
    row_count = nearby.shape[1]
    col_count = pieces.shape[2]

    def one_task(slot_index, running):
        amp_block = nearby[offsets[slot_index]]
        return running + jnp.dot(amp_block, pieces[slot_index], preferred_element_type=jnp.float32)

    start_sum = jnp.zeros((row_count, col_count), jnp.float32)
    return lax.fori_loop(begin_slot, end_slot, one_task, start_sum)


def body(amplitudes, integrals, cd_index, live_blocks, occ_energy, vir_energy):
    cycle_size = lax.axis_size("blk")
    here_index = lax.axis_index("blk")
    slot_count = integrals.shape[0]
    own_block = amplitudes[0]
    cycle_reach = REACH
    below_list = []
    above_list = []
    for stride in range(1, cycle_reach + 1):
        below_list.append(shifted(own_block, "blk", stride))
        above_list.append(shifted(own_block, "blk", -stride))
    nearby = jnp.stack(below_list[::-1] + [own_block] + above_list)
    my_live = live_blocks[here_index]
    my_cd = lax.dynamic_slice_in_dim(cd_index, here_index * slot_count, slot_count)
    my_offsets = cycle_offsets(my_cd, here_index, cycle_reach, cycle_size)
    denominator = vir_energy[0][None, :] - occ_energy[:, None]
    own_term = contract_tasks(nearby, integrals, my_offsets, 0, my_live)
    ladder = lax.psum_scatter(own_term, "grp", scatter_dimension=0, tiled=True)
    return (ladder / denominator)[None]


def solution(mesh):
    return jax.shard_map(
        body,
        mesh=mesh,
        in_specs=(P("blk", None, "grp"), P("blk", "grp", None), P(), P(), P("grp"), P("blk", None)),
        out_specs=P("blk", "grp", None),
        check_vma=False,
    )
```

profile of v0, /device:TPU:0, one launch (start us, length us, event | category | flops | bytes accessed | tf_op | source)
XLA Modules:
  0.0 109.3 jit_solution(11178116147794493922)
XLA Ops:
  6.5 0.0 reduce-scatter.2.cloned.1.call-start
  6.5 3.1 %collective-permute-start = (bf16[512,256]{1,0:T(8,128)(2,1)}, bf16[512,256]{1,0:T(8,128)(2,1)S(1)}, u32[]{:S(2)}, u32[]{:S(2)}) collective-permute-start(bf16[512,256]{1,0:T(8,128)(2,1)} %bitcast.26), channel_id=1, source_target_pairs={{0,8},{4,12},{8,16},{12,20},{16,24},{20,28},{24,0},{28,4},{1,9},{5... | collective-permute-start | bytes 786440 | tf_op jit(solution)/shard_map/ppermute | solution.py:12
  9.6 2.0 %collective-permute-start.3 = (bf16[512,256]{1,0:T(8,128)(2,1)}, bf16[512,256]{1,0:T(8,128)(2,1)S(1)}, u32[]{:S(2)}, u32[]{:S(2)}) collective-permute-start(bf16[512,256]{1,0:T(8,128)(2,1)} %bitcast.27), channel_id=1, source_target_pairs={{0,24},{4,28},{8,0},{12,4},{16,8},{20,12},{24,16},{28,20},{1,25},{... | collective-permute-start | bytes 786440 | tf_op jit(solution)/shard_map/ppermute | solution.py:12
  11.6 3.0 %collective-permute-start.2 = (bf16[512,256]{1,0:T(8,128)(2,1)}, bf16[512,256]{1,0:T(8,128)(2,1)S(1)}, u32[]{:S(2)}, u32[]{:S(2)}) collective-permute-start(bf16[512,256]{1,0:T(8,128)(2,1)} %bitcast.28), channel_id=1, source_target_pairs={{0,28},{4,0},{8,4},{12,8},{16,12},{20,16},{24,20},{28,24},{1,29},{... | collective-permute-start | bytes 786440 | tf_op jit(solution)/shard_map/ppermute | solution.py:12
  14.6 0.0 collective-permute-start.1
  14.6 0.7 and_select_fusion
  15.3 1.3 %dynamic_slice.15 = s32[1]{0:T(128)} dynamic-slice(s32[8]{0:T(128)} %param.11, s32[]{:T(128)S(6)} %select_n.20), dynamic_slice_sizes={1} | dynamic-slice | bytes 12 | tf_op jit(solution)/shard_map/dynamic_slice | solution.py:43
  16.6 2.4 %collective-permute-done = bf16[512,256]{1,0:T(8,128)(2,1)S(1)} collective-permute-done((bf16[512,256]{1,0:T(8,128)(2,1)}, bf16[512,256]{1,0:T(8,128)(2,1)S(1)}, u32[]{:S(2)}, u32[]{:S(2)}) %collective-permute-start) | collective-permute-done | bytes 262176 | tf_op jit(solution)/shard_map/ppermute | solution.py:12
  19.0 11.3 %collective-permute-done.1 = bf16[512,256]{1,0:T(8,128)(2,1)S(1)} collective-permute-done((bf16[512,256]{1,0:T(8,128)(2,1)}, bf16[512,256]{1,0:T(8,128)(2,1)S(1)}, u32[]{:S(2)}, u32[]{:S(2)}) %collective-permute-start.1) | collective-permute-done | bytes 262176 | tf_op jit(solution)/shard_map/ppermute | solution.py:12
  30.4 1.0 constant_dynamic-update-slice_fusion
  31.3 0.0 collective-permute-done.2
  31.4 0.0 collective-permute-done.3
  31.4 0.2 broadcast_in_dim.7
  31.7 24.4 %while.10 = (s32[]{:T(128)}, f32[512,1024]{1,0:T(8,128)S(1)}, s32[]{:T(128)}, s32[8]{0:T(128)S(1)}, bf16[5,512,256]{2,1,0:T(8,128)(2,1)S(1)}, /*index=5*/bf16[8,...) while((s32[]{:T(128)}, f32[512,1024]{1,0:T(8,128)S(1)}, s32[]{:T(128)}, ...), condition=%wide.region_1.2_spmd, body=%wide.region_0.1_spmd.sunk | while | flops 268959744 | bytes 4980933 | solution.py:28
  32.4 0.6 dynamic_slice.31
  34.9 1.5 %convolution_add_fusion.2 = f32[512,1024]{1,0:T(8,128)S(1)} fusion(f32[512,1024]{1,0:T(8,128)S(1)} %get-tuple-element.100, bf16[8,256,1024]{2,1,0:T(8,128)(2,1)} %get-tuple-element.114, s32[]{:T(128)S(6)} %select_n.26, bf16[5,512,256]{2,1,0:T(8,128)(2,1)S(1)} %get-tuple-element.113, s32[]{:T(128)S(6)} %select_n.27), kind=kOutput, calls=%fused_computation.clone.1 | convolution fusion | flops 268959744 | bytes 4980744 | tf_op jit(solution)/shard_map/while/body/dot_general | solution.py:25
  37.1 0.6 dynamic_slice.31
  39.6 1.5 %convolution_add_fusion.2 = f32[512,1024]{1,0:T(8,128)S(1)} fusion(f32[512,1024]{1,0:T(8,128)S(1)} %get-tuple-element.100, bf16[8,256,1024]{2,1,0:T(8,128)(2,1)} %get-tuple-element.114, s32[]{:T(128)S(6)} %select_n.26, bf16[5,512,256]{2,1,0:T(8,128)(2,1)S(1)} %get-tuple-element.113, s32[]{:T(128)S(6)} %select_n.27), kind=kOutput, calls=%fused_computation.clone.1 | convolution fusion | flops 268959744 | bytes 4980744 | tf_op jit(solution)/shard_map/while/body/dot_general | solution.py:25
  41.9 0.6 dynamic_slice.31
  44.4 1.5 %convolution_add_fusion.2 = f32[512,1024]{1,0:T(8,128)S(1)} fusion(f32[512,1024]{1,0:T(8,128)S(1)} %get-tuple-element.100, bf16[8,256,1024]{2,1,0:T(8,128)(2,1)} %get-tuple-element.114, s32[]{:T(128)S(6)} %select_n.26, bf16[5,512,256]{2,1,0:T(8,128)(2,1)S(1)} %get-tuple-element.113, s32[]{:T(128)S(6)} %select_n.27), kind=kOutput, calls=%fused_computation.clone.1 | convolution fusion | flops 268959744 | bytes 4980744 | tf_op jit(solution)/shard_map/while/body/dot_general | solution.py:25
  46.6 0.6 dynamic_slice.31
  49.1 1.5 %convolution_add_fusion.2 = f32[512,1024]{1,0:T(8,128)S(1)} fusion(f32[512,1024]{1,0:T(8,128)S(1)} %get-tuple-element.100, bf16[8,256,1024]{2,1,0:T(8,128)(2,1)} %get-tuple-element.114, s32[]{:T(128)S(6)} %select_n.26, bf16[5,512,256]{2,1,0:T(8,128)(2,1)S(1)} %get-tuple-element.113, s32[]{:T(128)S(6)} %select_n.27), kind=kOutput, calls=%fused_computation.clone.1 | convolution fusion | flops 268959744 | bytes 4980744 | tf_op jit(solution)/shard_map/while/body/dot_general | solution.py:25
  51.4 0.6 dynamic_slice.31
  53.9 1.5 %convolution_add_fusion.2 = f32[512,1024]{1,0:T(8,128)S(1)} fusion(f32[512,1024]{1,0:T(8,128)S(1)} %get-tuple-element.100, bf16[8,256,1024]{2,1,0:T(8,128)(2,1)} %get-tuple-element.114, s32[]{:T(128)S(6)} %select_n.26, bf16[5,512,256]{2,1,0:T(8,128)(2,1)S(1)} %get-tuple-element.113, s32[]{:T(128)S(6)} %select_n.27), kind=kOutput, calls=%fused_computation.clone.1 | convolution fusion | flops 268959744 | bytes 4980744 | tf_op jit(solution)/shard_map/while/body/dot_general | solution.py:25
  56.1 0.0 copy-start
  56.1 0.0 copy-start.1
  56.1 0.0 copy-start.2
  56.1 1.3 %copy-done = f32[512,1024]{1,0:T(8,128)} copy-done((f32[512,1024]{1,0:T(8,128)}, f32[512,1024]{1,0:T(8,128)S(1)}, u32[]{:S(2)}) %copy-start) | copy-done | bytes 2097176
  57.5 0.0 reduce-scatter.2.cloned.1.call-update
  57.5 43.0 %reduce-scatter.2.cloned.1.call-done = f32[128,1024]{1,0:T(8,128)} async-done(((f32[512,1024]{1,0:T(8,128)}), f32[128,1024]{1,0:T(8,128)}) %reduce-scatter.2.cloned.1.call-update) | async-done | bytes 524304 | tf_op jit(solution)/shard_map/reduce_scatter | solution.py:48
  100.5 0.0 copy-done.1
  100.5 0.0 copy-done.2
  100.5 2.0 %divide_bitcast_fusion = f32[1,128,1024]{2,1,0:T(8,128)} fusion(f32[128,1024]{1,0:T(8,128)} %reduce-scatter.2.cloned.1.call-done, f32[128]{0:T(128)S(1)} %copy-done.2, f32[1024]{0:T(1024)S(1)} %bitcast.30), kind=kLoop, calls=%fused_computation.6 | loop fusion | flops 262144 | bytes 1053184 | tf_op jit(solution)/shard_map/broadcast_in_dim | solution.py:49
  (4 shorter events, 0.1 us)
Async XLA Ops:
  6.5 94.0 %reduce-scatter.2.cloned.1.call-start = ((), (), s32[]{:S(2)}) async-start(), calls=%async_computation.1 | async-start | bytes 2621440 | tf_op jit(solution)/shard_map/reduce_scatter | solution.py:48
  6.5 12.5 %collective-permute-start = (bf16[512,256]{1,0:T(8,128)(2,1)}, bf16[512,256]{1,0:T(8,128)(2,1)S(1)}, u32[]{:S(2)}, u32[]{:S(2)}) collective-permute-start(bf16[512,256]{1,0:T(8,128)(2,1)} %bitcast.26), channel_id=1, source_target_pairs={{0,8},{4,12},{8,16},{12,20},{16,24},{20,28},{24,0},{28,4},{1,9},{5... | collective-permute-start | bytes 786440 | tf_op jit(solution)/shard_map/ppermute | solution.py:12
  9.6 21.8 %collective-permute-start.3 = (bf16[512,256]{1,0:T(8,128)(2,1)}, bf16[512,256]{1,0:T(8,128)(2,1)S(1)}, u32[]{:S(2)}, u32[]{:S(2)}) collective-permute-start(bf16[512,256]{1,0:T(8,128)(2,1)} %bitcast.27), channel_id=1, source_target_pairs={{0,24},{4,28},{8,0},{12,4},{16,8},{20,12},{24,16},{28,20},{1,25},{... | collective-permute-start | bytes 786440 | tf_op jit(solution)/shard_map/ppermute | solution.py:12
  11.6 19.7 %collective-permute-start.2 = (bf16[512,256]{1,0:T(8,128)(2,1)}, bf16[512,256]{1,0:T(8,128)(2,1)S(1)}, u32[]{:S(2)}, u32[]{:S(2)}) collective-permute-start(bf16[512,256]{1,0:T(8,128)(2,1)} %bitcast.28), channel_id=1, source_target_pairs={{0,28},{4,0},{8,4},{12,8},{16,12},{20,16},{24,20},{28,24},{1,29},{... | collective-permute-start | bytes 786440 | tf_op jit(solution)/shard_map/ppermute | solution.py:12
  14.6 15.8 %collective-permute-start.1 = (bf16[512,256]{1,0:T(8,128)(2,1)}, bf16[512,256]{1,0:T(8,128)(2,1)S(1)}, u32[]{:S(2)}, u32[]{:S(2)}) collective-permute-start(bf16[512,256]{1,0:T(8,128)(2,1)} %bitcast.29), channel_id=1, source_target_pairs={{0,4},{4,8},{8,12},{12,16},{16,20},{20,24},{24,28},{28,0},{1,5},{5... | collective-permute-start | bytes 786440 | tf_op jit(solution)/shard_map/ppermute | solution.py:12
  56.1 1.3 %copy-start = (f32[512,1024]{1,0:T(8,128)}, f32[512,1024]{1,0:T(8,128)S(1)}, u32[]{:S(2)}) copy-start(f32[512,1024]{1,0:T(8,128)S(1)} %get-tuple-element.38) | copy-start | bytes 6291460
  56.1 44.4 %copy-start.1 = (f32[1,1024]{1,0:T(1,128)S(1)}, f32[1,1024]{1,0:T(1,128)}, u32[]{:S(2)}) copy-start(f32[1,1024]{1,0:T(1,128)} %param.13) | copy-start | bytes 12292
  56.1 44.4 %copy-start.2 = (f32[128]{0:T(128)S(1)}, f32[128]{0:T(128)}, u32[]{:S(2)}) copy-start(f32[128]{0:T(128)} %param.12) | copy-start | bytes 1540
Sparse Core Ops, SparseCore 0:
  57.6 42.8 reduce-scatter.1
where the time goes:
time: 110 us; the launch traced here: 109 us
  waiting for transfers between devices  56.7 us (52%)
  loops' own time  13.6 us (12%)
  between operations  13.5 us (12%)
  starting transfers between devices  8.04 us (7%)
  matrix products  7.63 us (7%)
  local copies, waits for them, and re-layouts  7.1 us (6%)
  other arithmetic  2.71 us (2%)
    reduce_scatter x1, waiting for transfers between devices, body(): ladder = lax.psum_scatter(own_term, 'grp', scatter_dimension=0, tiled=True)  43 us
    ppermute x4, waiting for transfers between devices, shifted(): return lax.ppermute(value, axis, pairs)  13.7 us
    another operation x1, loops' own time, contract_tasks(): return lax.fori_loop(begin_slot, end_slot, one_task, start_sum)  13.6 us
    ppermute x4, starting transfers between devices, shifted(): return lax.ppermute(value, axis, pairs)  8.03 us
    dot_general x5, matrix products, one_task(): jnp.dot(amp_block, pieces[slot_index], preferred_element_type=jnp.float32)  7.63 us
    dynamic_slice x5, local copies, waits for them, and re-layouts, one_task(): amp_block = nearby[offsets[slot_index]]  3.19 us
    unnamed x10, local copies, waits for them, and re-layouts  2.35 us
  transfers between devices with their start and end apart: 5, of which 3 were waited for; matrix products, arithmetic and copies ran while one was open for 3% of the time, Pallas kernels for 0%

commit v1 on v0

v1 whole, which is shorter than its diff:
```python
import functools

import jax
import jax.numpy as jnp
from jax import lax
from jax.experimental import pallas as pl
from jax.experimental.pallas import tpu as pltpu
from jax.sharding import PartitionSpec as P

REACH = 2
PIECES = 2
TILE = 256
MESH = pl.DeviceIdType.MESH


def ladder_kernel(blocks, groups, cd_ref, live_ref, amp_ref, int_ref, out_ref, *scratch):
    slots, depth, cols = int_ref.shape
    rows = amp_ref.shape[1]
    halves = groups // 2
    owned = rows // groups
    piece = owned // PIECES
    steps = halves * PIECES
    far_steps = steps - PIECES
    window = 2 * REACH + 1
    near = scratch[:steps]
    (weights, own, pair_out, pair_in, far_out, far_in,
     amp_sem, int_sem, amp_send, amp_recv, pair_send, pair_recv, far_send, far_recv) = scratch[steps:]

    here = lax.axis_index("blk")
    me = lax.axis_index("grp")
    half, core = me // 2, me % 2
    mate = half * 2 + 1 - core
    offsets = [o for d in range(1, REACH + 1) for o in (d, -d)]

    amp_loads = []
    for step in range(steps):
        there = (half + step // PIECES + 1) % halves
        for part, side in enumerate((1 - core, core)):
            start = pl.multiple_of((there * 2 + side) * owned + (step % PIECES) * piece, piece)
            amp_loads.append(pltpu.make_async_copy(
                amp_ref.at[0, pl.ds(start, piece)],
                near[step].at[REACH, pl.ds(part * piece, piece)],
                amp_sem.at[step, part]))
    int_loads = [pltpu.make_async_copy(int_ref.at[k], weights.at[pl.ds(k * depth, depth)], int_sem.at[k])
                 for k in range(slots)]
    for load in amp_loads:
        load.start()
    for load in int_loads:
        load.start()

    barrier = pltpu.get_barrier_semaphore()
    for offset in offsets:
        pl.semaphore_signal(barrier, inc=1, device_id={"blk": (here - offset + blocks) % blocks}, device_id_type=MESH)
    pl.semaphore_signal(barrier, inc=1, device_id={"grp": mate}, device_id_type=MESH)
    for hop in range(1, halves):
        pl.semaphore_signal(barrier, inc=1, device_id={"grp": (half + hop) % halves * 2 + core}, device_id_type=MESH)
    for step in range(steps):
        near[step][window] = jnp.zeros(near[step].shape[1:], near[step].dtype)
    for load in amp_loads:
        load.wait()
    pl.semaphore_wait(barrier, len(offsets) + halves)

    amp_copies = {}
    for step in range(steps):
        for i, offset in enumerate(offsets):
            copy = pltpu.make_async_remote_copy(
                near[step].at[REACH], near[step].at[REACH + offset],
                amp_send.at[i, step], amp_recv.at[i, step],
                device_id={"blk": (here - offset + blocks) % blocks}, device_id_type=MESH)
            copy.start()
            amp_copies[i, step] = copy

    picks = []
    for k in range(slots):
        offset = (cd_ref[here * slots + k] - here + REACH + blocks) % blocks
        picks.append(jnp.where(k < live_ref[here], offset, window))

    pair_copies, far_copies = [], []

    def settle(step):
        pair_copies[step].wait_recv()
        if step < far_steps:
            far_out[step] = own[step] + pair_in[step]
            there = (half + step // PIECES + 1) % halves * 2 + core
            copy = pltpu.make_async_remote_copy(
                far_out.at[step], far_in.at[step], far_send.at[step], far_recv.at[step],
                device_id={"grp": there}, device_id_type=MESH)
            copy.start()
            far_copies.append(copy)

    for load in int_loads:
        load.wait()
    for step in range(steps):
        for i in range(len(offsets)):
            amp_copies[i, step].wait_recv()
        lhs = jnp.concatenate([near[step][pick] for pick in picks], axis=1)

        @pl.loop(0, cols // TILE)
        def _(tile):
            lanes = pl.ds(pl.multiple_of(tile * TILE, TILE), TILE)
            product = jnp.dot(lhs, weights[:, lanes], preferred_element_type=jnp.float32)
            pair_out[step, :, lanes] = product[:piece]
            own[step, :, lanes] = product[piece:]

        copy = pltpu.make_async_remote_copy(
            pair_out.at[step], pair_in.at[step], pair_send.at[step], pair_recv.at[step],
            device_id={"grp": mate}, device_id_type=MESH)
        copy.start()
        pair_copies.append(copy)
        if step >= 1:
            settle(step - 1)
    settle(steps - 1)
    for part in range(PIECES):
        total = own[far_steps + part] + pair_in[far_steps + part]
        for hop in range(halves - 1):
            far_copies[hop * PIECES + part].wait_recv()
            total = total + far_in[hop * PIECES + part]
        out_ref[pl.ds(part * piece, piece)] = total
    for copy in list(amp_copies.values()) + pair_copies + far_copies:
        copy.wait_send()


def body(blocks, groups, amplitudes, integrals, cd_index, live_blocks, occ_energy, vir_energy):
    slots, depth, cols = integrals.shape
    rows = amplitudes.shape[1]
    owned = rows // groups
    piece = owned // PIECES
    steps = groups // 2 * PIECES
    far_steps = steps - PIECES
    window = 2 * REACH + 1
    ladder = pl.pallas_call(
        functools.partial(ladder_kernel, blocks, groups),
        out_shape=jax.ShapeDtypeStruct((owned, cols), jnp.float32),
        in_specs=[pl.BlockSpec(memory_space=pltpu.SMEM)] * 2 + [pl.BlockSpec(memory_space=pl.ANY)] * 2,
        out_specs=pl.BlockSpec(memory_space=pltpu.VMEM),
        scratch_shapes=[pltpu.VMEM((window + 1, 2 * piece, depth), amplitudes.dtype)] * steps + [
            pltpu.VMEM((slots * depth, cols), integrals.dtype),
            pltpu.VMEM((steps, piece, cols), jnp.float32),
            pltpu.VMEM((steps, piece, cols), jnp.float32),
            pltpu.VMEM((steps, piece, cols), jnp.float32),
            pltpu.VMEM((far_steps, piece, cols), jnp.float32),
            pltpu.VMEM((far_steps, piece, cols), jnp.float32),
            pltpu.SemaphoreType.DMA((steps, 2)),
            pltpu.SemaphoreType.DMA((slots,)),
            pltpu.SemaphoreType.DMA((2 * REACH, steps)),
            pltpu.SemaphoreType.DMA((2 * REACH, steps)),
            pltpu.SemaphoreType.DMA((steps,)),
            pltpu.SemaphoreType.DMA((steps,)),
            pltpu.SemaphoreType.DMA((far_steps,)),
            pltpu.SemaphoreType.DMA((far_steps,)),
        ],
        compiler_params=pltpu.CompilerParams(
            collective_id=0, has_side_effects=True, vmem_limit_bytes=24 * 1024 * 1024),
    )(cd_index, live_blocks, amplitudes, integrals)
    denominator = vir_energy[0][None, :] - occ_energy[:, None]
    return (ladder / denominator)[None]


def solution(mesh):
    return jax.shard_map(
        functools.partial(body, mesh.shape["blk"], mesh.shape["grp"]),
        mesh=mesh,
        in_specs=(P("blk", None, "grp"), P("blk", "grp", None), P(), P(), P("grp"), P("blk", None)),
        out_specs=P("blk", "grp", None),
        check_vma=False,
    )
```

time: 110 us -> 36.8 us (0.33)
  waiting for transfers between devices: 56.7 us -> 0 us
  Pallas kernels: 0 us -> 31.1 us
  loops' own time: 13.6 us -> 0 us
  between operations: 13.5 us -> 0.03 us
  starting transfers between devices: 8.04 us -> 0 us
  matrix products: 7.63 us -> 0 us
  local copies, waits for them, and re-layouts: 7.1 us -> 4.47 us
  other arithmetic: 2.71 us -> 0.94 us
    reduce_scatter x1 -> x0, waiting for transfers between devices: 43 us -> none  [body(): ladder = lax.psum_scatter(own_term, 'grp', scatter_dimension=0, tiled=True)]
    pallas_call x0 -> x1, Pallas kernels: none -> 31.1 us  [body(): pl.pallas_call(functools.partial(ladder_kernel, blocks, groups), out_shap...]
    ppermute x4 -> x0, waiting for transfers between devices: 13.7 us -> none  [shifted(): return lax.ppermute(value, axis, pairs)]
    another operation x1 -> x0, loops' own time: 13.6 us -> none  [contract_tasks(): return lax.fori_loop(begin_slot, end_slot, one_task, start_sum)]
    ppermute x4 -> x0, starting transfers between devices: 8.03 us -> none  [shifted(): return lax.ppermute(value, axis, pairs)]
    dot_general x5 -> x0, matrix products: 7.63 us -> none  [one_task(): jnp.dot(amp_block, pieces[slot_index], preferred_element_type=jnp.float32)]
    dynamic_slice x6 -> x0, local copies, waits for them, and re-layouts: 4.49 us -> none  [the longest x5 3.19 us: one_task(): amp_block = nearby[offsets[slot_index]]]
    unnamed x10 -> x12, local copies, waits for them, and re-layouts: 2.35 us -> 4.47 us
  transfers between devices with their start and end apart: 5 -> 0, of which waited for: 3 -> 0; matrix products, arithmetic and copies ran while one was open for 3% -> 0% of each run, Pallas kernels for 0% -> 0%
where the time goes in v1:
time: 36.8 us; the launch traced here: 36.6 us
  Pallas kernels  31.1 us (85%)
  local copies, waits for them, and re-layouts  4.47 us (12%)
  other arithmetic  0.94 us (3%)
    pallas_call x1, Pallas kernels, body(): pl.pallas_call(functools.partial(ladder_kernel, blocks, groups), out_shap...  31.1 us
    unnamed x12, local copies, waits for them, and re-layouts  4.47 us
    broadcast_in_dim x1, other arithmetic, body(): return (ladder / denominator)[None]  0.94 us

profile of v1, /device:TPU:0, one launch (start us, length us, event | category | flops | bytes accessed | tf_op | source)
XLA Modules:
  0.0 36.6 jit_solution(8492450939960834677)
XLA Ops:
  0.0 0.0 copy-start.5
  0.0 0.0 copy-start
  0.0 2.2 %copy-done = bf16[8,256,1024]{2,1,0:T(8,128)(2,1)S(1)} copy-done((bf16[8,256,1024]{2,1,0:T(8,128)(2,1)S(1)}, bf16[8,256,1024]{2,1,0:T(8,128)(2,1)}, u32[]{:S(2)}) %copy-start) | copy-done | bytes 4194328
  2.2 0.0 copy-start.1
  2.2 0.9 %copy-done.1 = bf16[1,512,256]{2,1,0:T(8,128)(2,1)S(1)} copy-done((bf16[1,512,256]{2,1,0:T(8,128)(2,1)S(1)}, bf16[1,512,256]{2,1,0:T(8,128)(2,1)}, u32[]{:S(2)}) %copy-start.1) | copy-done | bytes 262168
  3.2 0.0 copy-start.2
  3.2 0.7 %copy-done.2 = s32[64]{0:T(128)S(1)} copy-done((s32[64]{0:T(128)S(1)}, s32[64]{0:T(128)}, u32[]{:S(2)}) %copy-start.2) | copy-done | bytes 280
  3.8 0.0 copy-start.3
  3.8 0.7 %copy-done.3 = s32[8]{0:T(128)S(1)} copy-done((s32[8]{0:T(128)S(1)}, s32[8]{0:T(128)}, u32[]{:S(2)}) %copy-start.3) | copy-done | bytes 56
  4.5 0.0 copy-start.4
  4.5 31.1 %shard_map.64 = f32[128,1024]{1,0:T(8,128)S(1)} custom-call(s32[64]{0:T(128)S(1)} %copy-done.2, s32[8]{0:T(128)S(1)} %copy-done.3, bf16[1,512,256]{2,1,0:T(8,128)(2,1)S(1)} %copy-done.1, bf16[8,256,1024]{2,1,0:T(8,128)(2,1)S(1)} %copy-done), custom_call_target="tpu_custom_call" | custom-call | tf_op jit(solution)/shard_map/pallas_call | solution.py:131
  35.6 0.0 copy-done.5
  35.6 0.0 copy-done.4
  35.6 0.9 %divide_bitcast_fusion = f32[1,128,1024]{2,1,0:T(8,128)} fusion(f32[128,1024]{1,0:T(8,128)S(1)} %shard_map.64, f32[128]{0:T(128)S(1)} %copy-done.5, f32[1024]{0:T(1024)S(1)} %bitcast.3), kind=kLoop, calls=%fused_computation | loop fusion | flops 262144 | bytes 1053184 | tf_op jit(solution)/shard_map/broadcast_in_dim | solution.py:156
Async XLA Ops:
  0.0 35.6 %copy-start.5 = (f32[128]{0:T(128)S(1)}, f32[128]{0:T(128)}, u32[]{:S(2)}) copy-start(f32[128]{0:T(128)} %param.10) | copy-start | bytes 1540
  0.0 2.2 %copy-start = (bf16[8,256,1024]{2,1,0:T(8,128)(2,1)S(1)}, bf16[8,256,1024]{2,1,0:T(8,128)(2,1)}, u32[]{:S(2)}) copy-start(bf16[8,256,1024]{2,1,0:T(8,128)(2,1)} %int_ref.1) | copy-start | bytes 12582916
  2.2 0.9 %copy-start.1 = (bf16[1,512,256]{2,1,0:T(8,128)(2,1)S(1)}, bf16[1,512,256]{2,1,0:T(8,128)(2,1)}, u32[]{:S(2)}) copy-start(bf16[1,512,256]{2,1,0:T(8,128)(2,1)} %amp_ref.1) | copy-start | bytes 786436
  3.2 0.7 %copy-start.2 = (s32[64]{0:T(128)S(1)}, s32[64]{0:T(128)}, u32[]{:S(2)}) copy-start(s32[64]{0:T(128)} %cd_ref.1) | copy-start | bytes 772
  3.8 0.7 %copy-start.3 = (s32[8]{0:T(128)S(1)}, s32[8]{0:T(128)}, u32[]{:S(2)}) copy-start(s32[8]{0:T(128)} %live_ref.1) | copy-start | bytes 100
  4.5 31.2 %copy-start.4 = (f32[1,1024]{1,0:T(1,128)S(1)}, f32[1,1024]{1,0:T(1,128)}, u32[]{:S(2)}) copy-start(f32[1,1024]{1,0:T(1,128)} %param.11) | copy-start | bytes 12292

commit v2 on v1

--- a/solution.py
+++ b/solution.py
@@ -8,7 +8,8 @@
 from jax.sharding import PartitionSpec as P
 
 REACH = 2
-PIECES = 2
+PIECES = 4
+AHEAD = 2
 TILE = 256
 MESH = pl.DeviceIdType.MESH
 
@@ -23,34 +24,36 @@
     far_steps = steps - PIECES
     window = 2 * REACH + 1
     near = scratch[:steps]
-    (weights, own, pair_out, pair_in, far_out, far_in,
+    (cd_smem, live_smem, table_sem, weights, own, pair_out, pair_in, far_out, far_in,
      amp_sem, int_sem, amp_send, amp_recv, pair_send, pair_recv, far_send, far_recv) = scratch[steps:]
 
     here = lax.axis_index("blk")
     me = lax.axis_index("grp")
     half, core = me // 2, me % 2
     mate = half * 2 + 1 - core
-    offsets = [o for d in range(1, REACH + 1) for o in (d, -d)]
+    side = 1 - 2 * (here % 2)
+    twin = here + side
 
     amp_loads = []
     for step in range(steps):
         there = (half + step // PIECES + 1) % halves
-        for part, side in enumerate((1 - core, core)):
-            start = pl.multiple_of((there * 2 + side) * owned + (step % PIECES) * piece, piece)
+        for part, lane in enumerate((1 - core, core)):
+            start = pl.multiple_of((there * 2 + lane) * owned + (step % PIECES) * piece, piece)
             amp_loads.append(pltpu.make_async_copy(
                 amp_ref.at[0, pl.ds(start, piece)],
                 near[step].at[REACH, pl.ds(part * piece, piece)],
                 amp_sem.at[step, part]))
     int_loads = [pltpu.make_async_copy(int_ref.at[k], weights.at[pl.ds(k * depth, depth)], int_sem.at[k])
                  for k in range(slots)]
-    for load in amp_loads:
-        load.start()
-    for load in int_loads:
+    table_loads = [pltpu.make_async_copy(cd_ref, cd_smem, table_sem.at[0]),
+                   pltpu.make_async_copy(live_ref, live_smem, table_sem.at[1])]
+    for load in amp_loads + int_loads + table_loads:
         load.start()
 
+    up, down = (here + REACH) % blocks, (here - REACH + blocks) % blocks
     barrier = pltpu.get_barrier_semaphore()
-    for offset in offsets:
-        pl.semaphore_signal(barrier, inc=1, device_id={"blk": (here - offset + blocks) % blocks}, device_id_type=MESH)
+    for target in (up, down, twin):
+        pl.semaphore_signal(barrier, inc=1, device_id={"blk": target}, device_id_type=MESH)
     pl.semaphore_signal(barrier, inc=1, device_id={"grp": mate}, device_id_type=MESH)
     for hop in range(1, halves):
         pl.semaphore_signal(barrier, inc=1, device_id={"grp": (half + hop) % halves * 2 + core}, device_id_type=MESH)
@@ -58,22 +61,44 @@
         near[step][window] = jnp.zeros(near[step].shape[1:], near[step].dtype)
     for load in amp_loads:
         load.wait()
-    pl.semaphore_wait(barrier, len(offsets) + halves)
+    pl.semaphore_wait(barrier, 3 + halves)
 
-    amp_copies = {}
+    def push(step, source, slot, lane, target):
+        return pltpu.make_async_remote_copy(
+            near[step].at[source], near[step].at[slot], amp_send.at[lane, step], amp_recv.at[slot, step],
+            device_id={"blk": target}, device_id_type=MESH)
+
+    def arrival(step, slot):
+        push(step, REACH, slot, 0, up).wait_recv()
+
+    sent = []
+
+    def launch(copy):
+        copy.start()
+        sent.append(copy)
+
+    def push_twin(step):
+        if step < steps:
+            launch(push(step, REACH, REACH - side, 2, twin))
+
+    def forward(step):
+        if step < steps:
+            arrival(step, REACH + 2 * side)
+            launch(push(step, REACH + 2 * side, REACH + side, 3, twin))
+            push_twin(step + AHEAD)
+
     for step in range(steps):
-        for i, offset in enumerate(offsets):
-            copy = pltpu.make_async_remote_copy(
-                near[step].at[REACH], near[step].at[REACH + offset],
-                amp_send.at[i, step], amp_recv.at[i, step],
-                device_id={"blk": (here - offset + blocks) % blocks}, device_id_type=MESH)
-            copy.start()
-            amp_copies[i, step] = copy
+        launch(push(step, REACH, 0, 0, up))
+        launch(push(step, REACH, 2 * REACH, 1, down))
+        if step < AHEAD:
+            push_twin(step)
 
+    for load in table_loads:
+        load.wait()
     picks = []
     for k in range(slots):
-        offset = (cd_ref[here * slots + k] - here + REACH + blocks) % blocks
-        picks.append(jnp.where(k < live_ref[here], offset, window))
+        offset = (cd_smem[here * slots + k] - here + REACH + blocks) % blocks
+        picks.append(jnp.where(k < live_smem[here], offset, window))
 
     pair_copies, far_copies = [], []
 
@@ -90,9 +115,11 @@
 
     for load in int_loads:
         load.wait()
+    forward(0)
     for step in range(steps):
-        for i in range(len(offsets)):
-            amp_copies[i, step].wait_recv()
+        forward(step + 1)
+        for slot in (REACH - 2 * side, REACH - side, REACH + side):
+            arrival(step, slot)
         lhs = jnp.concatenate([near[step][pick] for pick in picks], axis=1)
 
         @pl.loop(0, cols // TILE)
@@ -116,7 +143,7 @@
             far_copies[hop * PIECES + part].wait_recv()
             total = total + far_in[hop * PIECES + part]
         out_ref[pl.ds(part * piece, piece)] = total
-    for copy in list(amp_copies.values()) + pair_copies + far_copies:
+    for copy in sent + pair_copies + far_copies:
         copy.wait_send()
 
 
@@ -131,9 +158,12 @@
     ladder = pl.pallas_call(
         functools.partial(ladder_kernel, blocks, groups),
         out_shape=jax.ShapeDtypeStruct((owned, cols), jnp.float32),
-        in_specs=[pl.BlockSpec(memory_space=pltpu.SMEM)] * 2 + [pl.BlockSpec(memory_space=pl.ANY)] * 2,
+        in_specs=[pl.BlockSpec(memory_space=pltpu.HBM)] * 4,
         out_specs=pl.BlockSpec(memory_space=pltpu.VMEM),
         scratch_shapes=[pltpu.VMEM((window + 1, 2 * piece, depth), amplitudes.dtype)] * steps + [
+            pltpu.SMEM(cd_index.shape, cd_index.dtype),
+            pltpu.SMEM(live_blocks.shape, live_blocks.dtype),
+            pltpu.SemaphoreType.DMA((2,)),
             pltpu.VMEM((slots * depth, cols), integrals.dtype),
             pltpu.VMEM((steps, piece, cols), jnp.float32),
             pltpu.VMEM((steps, piece, cols), jnp.float32),
@@ -142,8 +172,8 @@
             pltpu.VMEM((far_steps, piece, cols), jnp.float32),
             pltpu.SemaphoreType.DMA((steps, 2)),
             pltpu.SemaphoreType.DMA((slots,)),
-            pltpu.SemaphoreType.DMA((2 * REACH, steps)),
-            pltpu.SemaphoreType.DMA((2 * REACH, steps)),
+            pltpu.SemaphoreType.DMA((4, steps)),
+            pltpu.SemaphoreType.DMA((window, steps)),
             pltpu.SemaphoreType.DMA((steps,)),
             pltpu.SemaphoreType.DMA((steps,)),
             pltpu.SemaphoreType.DMA((far_steps,)),
@@ -151,7 +181,7 @@
         ],
         compiler_params=pltpu.CompilerParams(
             collective_id=0, has_side_effects=True, vmem_limit_bytes=24 * 1024 * 1024),
-    )(cd_index, live_blocks, amplitudes, integrals)
+    )(*[pltpu.with_memory_space_constraint(x, pltpu.HBM) for x in (cd_index, live_blocks, amplitudes, integrals)])
     denominator = vir_energy[0][None, :] - occ_energy[:, None]
     return (ladder / denominator)[None]
 

time: 36.8 us -> 31.2 us (0.85)
  local copies, waits for them, and re-layouts: 4.47 us -> 0.01 us
  Pallas kernels: 31.1 us -> 30.1 us
    unnamed x12 -> x4, local copies, waits for them, and re-layouts: 4.47 us -> 0.01 us
    pallas_call x1, Pallas kernels: 31.1 us -> 30.1 us  [body(): pl.pallas_call(functools.partial(ladder_kernel, blocks, groups), out_shap...]
where the time goes in v2:
time: 31.2 us; the launch traced here: 31 us
  Pallas kernels  30.1 us (96%)
  other arithmetic  0.94 us (3%)
    pallas_call x1, Pallas kernels, body(): pl.pallas_call(functools.partial(ladder_kernel, blocks, groups), out_shap...  30.1 us
    broadcast_in_dim x1, other arithmetic, body(): return (ladder / denominator)[None]  0.94 us

profile of v2, /device:TPU:0, one launch (start us, length us, event | category | flops | bytes accessed | tf_op | source)
XLA Modules:
  0.0 31.0 jit_solution(4004018573695541771)
XLA Ops:
  0.0 0.0 copy-start
  0.0 0.0 copy-start.1
  0.0 30.1 %shard_map.64 = f32[128,1024]{1,0:T(8,128)S(1)} custom-call(s32[64]{0:T(128)} %cd_ref.1, s32[8]{0:T(128)} %live_ref.1, bf16[1,512,256]{2,1,0:T(8,128)(2,1)} %amp_ref.1, bf16[8,256,1024]{2,1,0:T(8,128)(2,1)} %int_ref.1), custom_call_target="tpu_custom_call" | custom-call | tf_op jit(solution)/shard_map/pallas_call | solution.py:158
  30.1 0.0 copy-done
  30.1 0.0 copy-done.1
  30.1 0.9 %divide_bitcast_fusion = f32[1,128,1024]{2,1,0:T(8,128)} fusion(f32[128,1024]{1,0:T(8,128)S(1)} %shard_map.64, f32[128]{0:T(128)S(1)} %copy-done.1, f32[1024]{0:T(1024)S(1)} %bitcast.3), kind=kLoop, calls=%fused_computation | loop fusion | flops 262144 | bytes 1053184 | tf_op jit(solution)/shard_map/broadcast_in_dim | solution.py:186
Async XLA Ops:
  0.0 30.1 %copy-start = (f32[1,1024]{1,0:T(1,128)S(1)}, f32[1,1024]{1,0:T(1,128)}, u32[]{:S(2)}) copy-start(f32[1,1024]{1,0:T(1,128)} %param.11) | copy-start | bytes 12292
  0.0 30.1 %copy-start.1 = (f32[128]{0:T(128)S(1)}, f32[128]{0:T(128)}, u32[]{:S(2)}) copy-start(f32[128]{0:T(128)} %param.10) | copy-start | bytes 1540

commit v3 on v2

--- a/solution.py
+++ b/solution.py
@@ -10,7 +10,7 @@
 REACH = 2
 PIECES = 4
 AHEAD = 2
-TILE = 256
+TILE = 512
 MESH = pl.DeviceIdType.MESH
 
 

time: 31.2 us -> 30.9 us (level)
  no operation moved by 1% of the time
where the time goes in v3:
time: 30.9 us; the launch traced here: 30.8 us
  Pallas kernels  29.8 us (96%)
  other arithmetic  0.94 us (3%)
    pallas_call x1, Pallas kernels, body(): pl.pallas_call(functools.partial(ladder_kernel, blocks, groups), out_shap...  29.8 us
    broadcast_in_dim x1, other arithmetic, body(): return (ladder / denominator)[None]  0.94 us

profile of v3, /device:TPU:0, one launch (start us, length us, event | category | flops | bytes accessed | tf_op | source)
XLA Modules:
  0.0 30.8 jit_solution(13488770267798503212)
XLA Ops:
  0.0 0.0 copy-start
  0.0 0.0 copy-start.1
  0.0 29.8 %shard_map.64 = f32[128,1024]{1,0:T(8,128)S(1)} custom-call(s32[64]{0:T(128)} %cd_ref.1, s32[8]{0:T(128)} %live_ref.1, bf16[1,512,256]{2,1,0:T(8,128)(2,1)} %amp_ref.1, bf16[8,256,1024]{2,1,0:T(8,128)(2,1)} %int_ref.1), custom_call_target="tpu_custom_call" | custom-call | tf_op jit(solution)/shard_map/pallas_call | solution.py:158
  29.8 0.0 copy-done
  29.8 0.0 copy-done.1
  29.8 0.9 %divide_bitcast_fusion = f32[1,128,1024]{2,1,0:T(8,128)} fusion(f32[128,1024]{1,0:T(8,128)S(1)} %shard_map.64, f32[128]{0:T(128)S(1)} %copy-done.1, f32[1024]{0:T(1024)S(1)} %bitcast.3), kind=kLoop, calls=%fused_computation | loop fusion | flops 262144 | bytes 1053184 | tf_op jit(solution)/shard_map/broadcast_in_dim | solution.py:186
Async XLA Ops:
  0.0 29.8 %copy-start = (f32[1,1024]{1,0:T(1,128)S(1)}, f32[1,1024]{1,0:T(1,128)}, u32[]{:S(2)}) copy-start(f32[1,1024]{1,0:T(1,128)} %param.11) | copy-start | bytes 12292
  0.0 29.8 %copy-start.1 = (f32[128]{0:T(128)S(1)}, f32[128]{0:T(128)}, u32[]{:S(2)}) copy-start(f32[128]{0:T(128)} %param.10) | copy-start | bytes 1540
